TPU v7x, 256 devices: a whole 4x4x8 slice. The times are simulated.
256 devices in a mesh: member: 16 (over y_lo, x, core), dp: 16 (over z, y_hi).
Axes of the slice: x: 4, y: 4 (y_hi: 2, y_lo: 2; y = y_hi * 2 + y_lo), z: 8, core: 2. Of those that a mesh axis runs over, the one named last changes fastest.
Arguments:
- trunk: bfloat16 [6304, 1024], P('dp'), may hold values from -6 to 6
- normgain: float32 [1024], replicated, may hold values from 0.25 to 1.75
- expand: bfloat16 [1024, 2048], P('member'), may hold values from -0.1875 to 0.1875
- shrink: bfloat16 [2048, 1024], P('member'), may hold values from -0.125 to 0.125
- inscale: float32 [16, 1024], P('member'), may hold values from 0.25 to 1.75
- hidscale: float32 [16, 2048], P('member'), may hold values from 0.25 to 1.75
- actscale: float32 [16, 2048], P('member'), may hold values from 0.25 to 1.75
- outscale: float32 [16, 1024], P('member'), may hold values from 0.25 to 1.75
- cotangent: bfloat16 [16, 6304, 1024], P('member', 'dp'), may hold values from -6 to 6
Outputs:
- trunk_grad: bfloat16 [6304, 1024], P('dp', 'member')
- expand_grad: float32 [1024, 2048], P('member')
- shrink_grad: float32 [2048, 1024], P('member')
- inscale_grad: float32 [16, 1024], P('member')
- hidscale_grad: float32 [16, 2048], P('member')
- actscale_grad: float32 [16, 2048], P('member')
- outscale_grad: float32 [16, 1024], P('member')
- normgain_grad: float32 [1024], replicated
All inputs are finite; a program needn't handle non-finite values.
Results may differ from a plain program's by a relative error of at most 0.024.
Values may be sent and summed in bfloat16 or wider, within the bound.
A program may use at most 64 MiB of HBM per device.

v0:
```python
import jax
import jax.numpy as jnp
from jax import lax
from jax.sharding import Mesh
from jax.sharding import PartitionSpec as P

MEMBER = ("member_0", "member_1", "member_2")
eps = 1e-06
coeff = 0.7978845608028654


def sent_to_all(x, axis):
    copies = jnp.broadcast_to(x, (lax.axis_size(axis), *x.shape))
    return lax.all_to_all(copies, axis, split_axis=0, concat_axis=0, tiled=True)


def joined_along(tiles, dim):
    tiles = jnp.moveaxis(tiles, 0, dim)
    dims = tiles.shape
    return tiles.reshape(*dims[:dim], dims[dim] * dims[dim + 1], *dims[dim + 2 :])


def gathered_by_axis(x, axes, dim):
    far, near = axes
    tiles = sent_to_all(sent_to_all(x, far), near)
    return joined_along(tiles.swapaxes(0, 1).reshape(-1, *x.shape), dim)


def split_up(x, dim, peers):
    before, after = (x.shape[:dim], x.shape[dim + 1 :])
    return jnp.moveaxis(x.reshape(*before, peers, -1, *after), dim, 0)


def sent_and_summed(x, axis, dim):
    tiles = split_up(x, dim, lax.axis_size(axis))
    arrived = lax.all_to_all(tiles, axis, split_axis=0, concat_axis=0, tiled=True)
    return arrived.astype(jnp.float32).sum(axis=0)


def summed_rows(x, axes, dim):
    far, near = axes
    tiles = split_up(x, dim, lax.axis_size(far))
    nearer = sent_and_summed(tiles, near, dim + 1)
    arrived = lax.all_to_all(
        nearer.astype(jnp.bfloat16), far, split_axis=0, concat_axis=0, tiled=True
    )
    return arrived.astype(jnp.float32).sum(axis=0)


def filled_up(lines, peers):
    spare = -len(lines) % peers
    return jnp.pad(lines, [(0, spare)] + [(0, 0)] * (lines.ndim - 1))


def collect(x, axis, dim):
    return joined_along(sent_to_all(x, axis), dim)


def sum_by_parts(x, axes):
    lines = x.reshape(-1, x.shape[-1])
    own = sent_and_summed(filled_up(lines, lax.axis_size(axes)), axes, 0)
    whole = collect(own.astype(jnp.bfloat16), axes, 0)
    return whole[: len(lines)].reshape(x.shape).astype(jnp.float32)


def over_copies(x, axis):
    return sent_to_all(x, axis).sum(axis=0)


def in_one(arrays, axis):
    ends = [0]
    for a in arrays:
        ends.append(ends[-1] + a.size)
    total = over_copies(jnp.concatenate([a.ravel() for a in arrays]), axis)
    return tuple((total[b:e].reshape(a.shape) for a, b, e in zip(arrays, ends, ends[1:])))


def gelu_pair(hidden):
    inner = coeff * (hidden + 0.044715 * hidden * hidden * hidden)
    tangent = jnp.tanh(inner)
    active = 0.5 * hidden * (1.0 + tangent)
    slope = 0.5 * (1.0 + tangent) + 0.5 * hidden * (1.0 - tangent * tangent) * coeff * (
        1.0 + 3.0 * 0.044715 * hidden * hidden
    )
    return (active, slope)


def rounded_term(left, right):
    term = lax.dot_general(
        left, right, (((0,), (0,)), ((), ())), preferred_element_type=jnp.float32
    )
    return lax.optimization_barrier(term.astype(jnp.bfloat16)).astype(jnp.float32)


def body(trunk, normgain, expand, shrink, inscale, hidscale, actscale, outscale, cotangent):
    scale_in = inscale[0]
    scale_hid = hidscale[0]
    scale_act = actscale[0]
    scale_out = outscale[0]
    tokens = trunk.astype(jnp.float32)
    centered = tokens - jnp.mean(tokens, axis=1, keepdims=True)
    variance = jnp.mean(centered * centered, axis=1, keepdims=True)
    inv_std = lax.rsqrt(variance + eps)
    normed = centered * inv_std
    gained = normed * normgain
    scaled_in = (gained * scale_in).astype(jnp.bfloat16)
    expand_full = lax.all_gather(expand, MEMBER, axis=0, tiled=True)
    project = jnp.dot(scaled_in, expand_full, preferred_element_type=jnp.float32)
    hidden = project * scale_hid
    active, slope = gelu_pair(hidden)
    scaled_act = (active * scale_act).astype(jnp.bfloat16)
    upstream = cotangent[0].astype(jnp.float32)
    scaled_cot = (upstream * scale_out).astype(jnp.bfloat16)
    piece = gathered_by_axis(shrink, (("member_0", "member_1"), "member_2"), 0)
    second = jnp.dot(scaled_act, piece, preferred_element_type=jnp.float32)
    back = lax.dot_general(
        scaled_cot, piece, (((1,), (1,)), ((), ())), preferred_element_type=jnp.float32
    )
    back_act = back
    second, back_act = (second, back_act)
    grad_out = jnp.sum(upstream * second, axis=0)
    grad_act = jnp.sum(back_act * active, axis=0)
    back_hidden = back_act * scale_act * slope
    grad_hid = jnp.sum(back_hidden * project, axis=0)
    back_proj = (back_hidden * scale_hid).astype(jnp.bfloat16)
    expand_part = summed_rows(
        rounded_term(scaled_in, back_proj).astype(jnp.bfloat16),
        (("member_0", "member_1"), "member_2"),
        0,
    )
    shrink_part = summed_rows(
        rounded_term(scaled_act, scaled_cot).astype(jnp.bfloat16),
        (("member_0", "member_1"), "member_2"),
        0,
    )
    expand_grad, shrink_grad = (
        sum_by_parts(expand_part.astype(jnp.bfloat16), "dp"),
        sum_by_parts(shrink_part.astype(jnp.bfloat16), "dp"),
    )
    back_norm = lax.dot_general(
        back_proj, expand_full, (((1,), (1,)), ((), ())), preferred_element_type=jnp.float32
    )
    grad_in = jnp.sum(back_norm * gained, axis=0)
    back_scaled = back_norm * scale_in
    gain_term = jnp.sum(back_scaled * normed, axis=0)
    back_unit = back_scaled * normgain
    back_trunk = inv_std * (
        back_unit
        - jnp.mean(back_unit, axis=1, keepdims=True)
        - normed * jnp.mean(back_unit * normed, axis=1, keepdims=True)
    )
    member_term = upstream + back_trunk
    trunk_grad = sent_and_summed(member_term.astype(jnp.bfloat16), MEMBER, 1).astype(jnp.bfloat16)
    grad_in, grad_hid, grad_act, grad_out, gain_shard = in_one(
        (grad_in, grad_hid, grad_act, grad_out, gain_term), "dp"
    )
    gain_grad = over_copies(gain_shard, MEMBER)
    return (
        trunk_grad,
        expand_grad,
        shrink_grad,
        grad_in[None],
        grad_hid[None],
        grad_act[None],
        grad_out[None],
        gain_grad,
    )


def solution(mesh):
    finer = Mesh(
        mesh.devices.reshape(2, 4, 2, mesh.shape["dp"]), ("member_0", "member_1", "member_2", "dp")
    )
    in_specs = (
        P("dp", None),
        P(),
        P(MEMBER, None),
        P(MEMBER, None),
        P(MEMBER, None),
        P(MEMBER, None),
        P(MEMBER, None),
        P(MEMBER, None),
        P(MEMBER, "dp", None),
    )
    out_specs = (
        P("dp", MEMBER),
        P(MEMBER, None),
        P(MEMBER, None),
        P(MEMBER, None),
        P(MEMBER, None),
        P(MEMBER, None),
        P(MEMBER, None),
        P(),
    )
    return jax.shard_map(body, mesh=finer, in_specs=in_specs, out_specs=out_specs, check_vma=False)
```

profile of v0, /device:TPU:8, one launch (start us, length us, event | category | flops | bytes accessed | tf_op | source)
XLA Modules:
  0.0 317.4 jit_solution(12734090389983294515)
XLA Ops:
  7.2 0.0 all-gather.2.cloned.1.call-start
  7.2 0.7 all-gather.2.cloned.1.call-update
  7.9 2.6 broadcast_in_dim.36
  10.5 5.8 %all-to-all-start = ((bf16[8,128,1024]{2,1,0:T(8,128)(2,1)}), bf16[8,128,1024]{2,1,0:T(8,128)(2,1)S(1)}, u32[]{:S(2)}, u32[]{:S(2)}) async-start(bf16[8,128,1024]{2,1,0:T(8,128)(2,1)} %broadcast_in_dim.36), calls=%async_computation | async-start | bytes 4194304 | tf_op jit(solution)/shard_map/all_to_all | solution.py:14
  16.3 0.0 copy-done.1
  16.3 0.2 convert_reduce_fusion
  16.5 0.4 fusion.23
  16.9 27.5 %all-to-all-done = bf16[8,128,1024]{2,1,0:T(8,128)(2,1)S(1)} async-done(((bf16[8,128,1024]{2,1,0:T(8,128)(2,1)}), bf16[8,128,1024]{2,1,0:T(8,128)(2,1)S(1)}, u32[]{:S(2)}, u32[]{:S(2)}) %all-to-all-start) | async-done | bytes 2097184 | tf_op jit(solution)/shard_map/all_to_all | solution.py:14
  44.3 0.5 broadcast_in_dim.37
  44.8 7.5 %all_to_all.67 = bf16[2,8,128,1024]{3,2,1,0:T(8,128)(2,1)S(1)} all-to-all(bf16[2,8,128,1024]{3,2,1,0:T(8,128)(2,1)S(1)} %broadcast_in_dim.37), channel_id=1, replica_groups=mesh['member_0'=2,'member_1'=4,'member_2'=2,'dp'=16] {'member_2'}, dimensions={0} | all-to-all | bytes 8388608 | tf_op jit(solution)/shard_map/all_to_all | solution.py:14
  52.4 2.4 copy.27
  54.8 10.6 %all-gather.2.cloned.1.call-done = bf16[1024,2048]{1,0:T(8,128)(2,1)} async-done(((bf16[64,2048]{1,0:T(8,128)(2,1)}), bf16[1024,2048]{1,0:T(8,128)(2,1)}) %all-gather.2.cloned.1.call-update) | async-done | bytes 4194320 | tf_op jit(solution)/shard_map/all_gather | solution.py:107
  65.4 0.0 copy-start.7
  65.4 0.0 copy-start.8
  65.4 4.3 %fusion.37 = f32[394,2048]{1,0:T(8,128)S(1)} fusion(bf16[1024,2048]{1,0:T(8,128)(2,1)} %all-gather.2.cloned.1.call-done, bf16[394,1024]{1,0:T(8,128)(2,1)S(1)} %copy-done.1, f32[1024]{0:T(1024)S(1)} %bitcast.60, f32[1024]{0:T(1024)S(1)} %copy-done.5, f32[394]{0:T(512)S(1)} %add_rsqrt_fusion, f32[394]{0:T(512)S(1)} %broadcast_multiply_fusion.2), kind=kOutput, calls=%fused_computation.60 | convolution fusion | flops 1654976512 | bytes 8240208 | tf_op jit(solution)/shard_map/dot_general | solution.py:108
  69.7 0.0 copy-start.9
  69.8 2.4 fusion.26
  72.2 4.2 %multiply_reduce_fusion = (f32[2048]{0:T(1024)S(1)}, f32[2048]{0:T(1024)S(1)}, f32[394,2048]{1,0:T(8,128)S(1)}) fusion(f32[394,2048]{1,0:T(8,128)S(1)} %fusion.37, f32[2048]{0:T(1024)S(1)} %bitcast.65, f32[2048]{0:T(1024)S(1)} %bitcast.70, bf16[2048,1024]{1,0:T(8,128)(2,1)S(1)} %bitcast.55, bf16[1,394,1024]{2,1,0:T(8,128)(2,1)S(1)} %copy-done.3, ...), kind=kOutput, calls=%fused_computation.12 | convolution fusion | flops 1673934848 | bytes 11493376 | tf_op jit(solution)/shard_map/dot_general | solution.py:116
  76.4 5.0 %convolution_convert_fusion = bf16[2048,1024]{1,0:T(8,128)(2,1)} fusion(bf16[1,394,1024]{2,1,0:T(8,128)(2,1)S(1)} %copy-done.3, f32[1024]{0:T(1024)S(1)} %bitcast.75, f32[2048]{0:T(1024)S(1)} %bitcast.71, f32[394,2048]{1,0:T(8,128)S(1)} %fusion.37, f32[2048]{0:T(1024)S(1)} %bitcast.66), kind=kOutput, calls=%fused_computation.4 | convolution fusion | flops 1664739328 | bytes 8249344 | tf_op jit(solution)/shard_map/dot_general | solution.py:89
  81.4 4.5 %convolution_convert_fusion.1 = bf16[1024,2048]{1,0:T(8,128)(2,1)S(1)} fusion(f32[2048]{0:T(1024)S(1)} %bitcast.67, bf16[394,1024]{1,0:T(8,128)(2,1)S(1)} %copy-done.1, f32[1024]{0:T(1024)S(1)} %bitcast.61, f32[1024]{0:T(1024)S(1)} %copy-done.5, f32[394]{0:T(512)S(1)} %add_rsqrt_fusion, f32[394]{0:T(512)S(1)} %broadcast_multiply_fusion.2, ...), kind=kOutput, calls=%fused_computation.5 | convolution fusion | flops 1674825728 | bytes 11484240 | tf_op jit(solution)/shard_map/dot_general | solution.py:89
  85.9 5.2 %fusion.22 = (f32[1024]{0:T(1024)S(1)}, f32[394]{0:T(512)S(1)}, f32[1024]{0:T(1024)S(1)}, f32[394]{0:T(512)S(1)}, f32[394,1024]{1,0:T(8,128)}) fusion(bf16[394,1024]{1,0:T(8,128)(2,1)S(1)} %copy-done.1, f32[1024]{0:T(1024)S(1)} %bitcast.62, f32[394]{0:T(512)S(1)} %add_rsqrt_fusion, f32[394]{0:T(512)S(1)} %broadcast_multiply_fusion.2, ...), kind=kOutput, calls=%fused_computation.37 | convolution fusion | flops 1675549952 | bytes 13109408 | tf_op jit(solution)/shard_map/dot_general | solution.py:140
  91.1 2.3 copy.45
  93.4 5.6 %all-to-all-start.3 = ((bf16[2,8,64,2048]{3,2,1,0:T(8,128)(2,1)}), bf16[2,8,64,2048]{3,2,1,0:T(8,128)(2,1)}, u32[]{:S(2)}, u32[]{:S(2)}) async-start(bf16[2,8,64,2048]{3,2,1,0:T(8,128)(2,1)} %bitcast.50), calls=%async_computation.3 | async-start | bytes 8388608 | tf_op jit(solution)/shard_map/all_to_all | solution.py:36
  99.0 4.8 %copy.44 = bf16[8,2,128,1024]{3,2,0,1:T(8,128)(2,1)} copy(bf16[8,2,128,1024]{3,2,1,0:T(8,128)(2,1)} %bitcast.52) | data formatting | bytes 8388608 | tf_op jit(solution)/shard_map/reshape;reshape | solution.py:31
  103.8 0.0 all-to-all-done.3
  103.8 11.9 %all_to_all.68 = bf16[2,8,128,1024]{3,2,1,0:T(8,128)(2,1)} all-to-all(bf16[2,8,128,1024]{3,2,1,0:T(8,128)(2,1)} %bitcast.51), channel_id=1, replica_groups=mesh['member_0'=2,'member_1'=4,'member_2'=2,'dp'=16] {'member_2'}, dimensions={0} | all-to-all | bytes 8388608 | tf_op jit(solution)/shard_map/all_to_all | solution.py:36
  115.7 1.0 broadcast_in_dim.40
  116.7 10.2 %all-to-all-start.11 = ((f32[16,1,7168]{2,1,0:T(1,128)}), f32[16,1,7168]{2,1,0:T(1,128)S(1)}, u32[]{:S(2)}, u32[]{:S(2)}) async-start(f32[16,1,7168]{2,1,0:T(1,128)} %broadcast_in_dim.40), calls=%async_computation.11 | async-start | bytes 917504 | tf_op jit(solution)/shard_map/all_to_all | solution.py:14
  126.9 2.2 fusion.24
  129.1 1.4 copy.28
  130.4 14.5 %all-to-all-done.11 = f32[16,1,7168]{2,1,0:T(1,128)S(1)} async-done(((f32[16,1,7168]{2,1,0:T(1,128)}), f32[16,1,7168]{2,1,0:T(1,128)S(1)}, u32[]{:S(2)}, u32[]{:S(2)}) %all-to-all-start.11) | async-done | bytes 458784 | tf_op jit(solution)/shard_map/all_to_all | solution.py:14
  145.0 5.4 %all-to-all-start.2 = ((bf16[16,394,64]{1,2,0:T(8,128)(2,1)}), bf16[16,394,64]{1,2,0:T(8,128)(2,1)S(1)}, u32[]{:S(2)}, u32[]{:S(2)}) async-start(bf16[16,394,64]{1,2,0:T(8,128)(2,1)} %bitcast.9), calls=%async_computation.2 | async-start | bytes 2097152 | tf_op jit(solution)/shard_map/all_to_all | solution.py:36
  150.4 0.3 reduce_sum.199
  150.7 0.6 fusion.41
  151.3 14.2 %all-to-all-done.2 = bf16[16,394,64]{1,2,0:T(8,128)(2,1)S(1)} async-done(((bf16[16,394,64]{1,2,0:T(8,128)(2,1)}), bf16[16,394,64]{1,2,0:T(8,128)(2,1)S(1)}, u32[]{:S(2)}, u32[]{:S(2)}) %all-to-all-start.2) | async-done | bytes 806944 | tf_op jit(solution)/shard_map/all_to_all | solution.py:36
  165.5 0.7 broadcast_in_dim.45
  166.2 4.9 %all-to-all-start.12 = ((f32[16,1,1024]{2,1,0:T(1,128)}), f32[16,1,1024]{2,1,0:T(1,128)S(1)}, u32[]{:S(2)}, u32[]{:S(2)}) async-start(f32[16,1,1024]{2,1,0:T(1,128)} %broadcast_in_dim.45), calls=%async_computation.12 | async-start | bytes 131072 | tf_op jit(solution)/shard_map/all_to_all | solution.py:14
  171.0 5.2 %reduce_sum.188 = bf16[8,64,2048]{2,1,0:T(8,128)(2,1)} reduce(bf16[2,8,64,2048]{3,2,1,0:T(8,128)(2,1)} %all-to-all-done.3, bf16[]{:T(256)} %constant.28.clone.1), dimensions={0}, to_apply=%region_5.0 | reduce | flops 1048576 | bytes 6291458 | tf_op jit(solution)/shard_map/reduce_sum | solution.py:37
  176.2 0.0 all-to-all-done.12
  176.2 5.7 %all-to-all-start.4 = ((bf16[8,64,2048]{2,1,0:T(8,128)(2,1)}), bf16[8,64,2048]{2,1,0:T(8,128)(2,1)S(1)}, u32[]{:S(2)}, u32[]{:S(2)}) async-start(bf16[8,64,2048]{2,1,0:T(8,128)(2,1)} %reduce_sum.188), calls=%async_computation.4 | async-start | bytes 4194304 | tf_op jit(solution)/shard_map/all_to_all | solution.py:44
  181.9 5.2 %reduce_sum.191 = bf16[8,128,1024]{2,1,0:T(8,128)(2,1)} reduce(bf16[2,8,128,1024]{3,2,1,0:T(8,128)(2,1)} %all_to_all.68, bf16[]{:T(256)} %constant.28.clone.1), dimensions={0}, to_apply=%region_8.0 | reduce | flops 1048576 | bytes 6291458 | tf_op jit(solution)/shard_map/reduce_sum | solution.py:37
  187.2 20.5 %all-to-all-done.4 = bf16[8,64,2048]{2,1,0:T(8,128)(2,1)S(1)} async-done(((bf16[8,64,2048]{2,1,0:T(8,128)(2,1)}), bf16[8,64,2048]{2,1,0:T(8,128)(2,1)S(1)}, u32[]{:S(2)}, u32[]{:S(2)}) %all-to-all-start.4) | async-done | bytes 2097184 | tf_op jit(solution)/shard_map/all_to_all | solution.py:44
  207.7 1.3 copy-done
  209.0 8.7 %all-to-all-start.8 = ((bf16[8,128,1024]{2,1,0:T(8,128)(2,1)}), bf16[8,128,1024]{2,1,0:T(8,128)(2,1)S(1)}, u32[]{:S(2)}, u32[]{:S(2)}) async-start(bf16[8,128,1024]{2,1,0:T(8,128)(2,1)} %reduce_sum.191), calls=%async_computation.8 | async-start | bytes 4194304 | tf_op jit(solution)/shard_map/all_to_all | solution.py:44
  217.7 2.0 reduce_sum.189
  219.6 0.8 reshape.70
  220.4 21.8 %all-to-all-done.8 = bf16[8,128,1024]{2,1,0:T(8,128)(2,1)S(1)} async-done(((bf16[8,128,1024]{2,1,0:T(8,128)(2,1)}), bf16[8,128,1024]{2,1,0:T(8,128)(2,1)S(1)}, u32[]{:S(2)}, u32[]{:S(2)}) %all-to-all-start.8) | async-done | bytes 2097184 | tf_op jit(solution)/shard_map/all_to_all | solution.py:44
  242.2 3.5 %all-to-all-start.5 = ((bf16[16,4,2048]{2,1,0:T(4,128)(2,1)}), bf16[16,4,2048]{2,1,0:T(4,128)(2,1)S(1)}, u32[]{:S(2)}, u32[]{:S(2)}) async-start(bf16[16,4,2048]{2,1,0:T(4,128)(2,1)} %reshape.70), calls=%async_computation.5 | async-start | bytes 524288 | tf_op jit(solution)/shard_map/all_to_all | solution.py:36
  245.8 1.1 reduce_sum.192
  246.9 13.0 %all-to-all-done.5 = bf16[16,4,2048]{2,1,0:T(4,128)(2,1)S(1)} async-done(((bf16[16,4,2048]{2,1,0:T(4,128)(2,1)}), bf16[16,4,2048]{2,1,0:T(4,128)(2,1)S(1)}, u32[]{:S(2)}, u32[]{:S(2)}) %all-to-all-start.5) | async-done | bytes 262176 | tf_op jit(solution)/shard_map/all_to_all | solution.py:36
  259.9 3.5 %all-to-all-start.9 = ((bf16[16,8,1024]{2,1,0:T(8,128)(2,1)}), bf16[16,8,1024]{2,1,0:T(8,128)(2,1)S(1)}, u32[]{:S(2)}, u32[]{:S(2)}) async-start(bf16[16,8,1024]{2,1,0:T(8,128)(2,1)} %bitcast.14), calls=%async_computation.9 | async-start | bytes 524288 | tf_op jit(solution)/shard_map/all_to_all | solution.py:36
  263.4 0.1 reduce_sum.190
  263.5 12.4 %all-to-all-done.9 = bf16[16,8,1024]{2,1,0:T(8,128)(2,1)S(1)} async-done(((bf16[16,8,1024]{2,1,0:T(8,128)(2,1)}), bf16[16,8,1024]{2,1,0:T(8,128)(2,1)S(1)}, u32[]{:S(2)}, u32[]{:S(2)}) %all-to-all-start.9) | async-done | bytes 262176 | tf_op jit(solution)/shard_map/all_to_all | solution.py:36
  276.0 0.8 broadcast_in_dim.38
  276.8 3.5 %all-to-all-start.6 = ((bf16[16,4,2048]{2,1,0:T(4,128)(2,1)}), bf16[16,4,2048]{2,1,0:T(4,128)(2,1)S(1)}, u32[]{:S(2)}, u32[]{:S(2)}) async-start(bf16[16,4,2048]{2,1,0:T(4,128)(2,1)} %broadcast_in_dim.38), calls=%async_computation.6 | async-start | bytes 524288 | tf_op jit(solution)/shard_map/all_to_all | solution.py:14
  280.4 12.5 %all-to-all-done.6 = bf16[16,4,2048]{2,1,0:T(4,128)(2,1)S(1)} async-done(((bf16[16,4,2048]{2,1,0:T(4,128)(2,1)}), bf16[16,4,2048]{2,1,0:T(4,128)(2,1)S(1)}, u32[]{:S(2)}, u32[]{:S(2)}) %all-to-all-start.6) | async-done | bytes 262176 | tf_op jit(solution)/shard_map/all_to_all | solution.py:14
  292.8 0.7 broadcast_in_dim.39
  293.6 3.5 %all-to-all-start.10 = ((bf16[16,8,1024]{2,1,0:T(8,128)(2,1)}), bf16[16,8,1024]{2,1,0:T(8,128)(2,1)S(1)}, u32[]{:S(2)}, u32[]{:S(2)}) async-start(bf16[16,8,1024]{2,1,0:T(8,128)(2,1)} %broadcast_in_dim.39), calls=%async_computation.10 | async-start | bytes 524288 | tf_op jit(solution)/shard_map/all_to_all | solution.py:14
  297.1 0.8 reduce_sum.187
  297.9 0.6 fusion.42
  298.5 0.6 reduce_sum.200
  299.2 0.8 reshape.73
  300.0 9.7 %all-to-all-done.10 = bf16[16,8,1024]{2,1,0:T(8,128)(2,1)S(1)} async-done(((bf16[16,8,1024]{2,1,0:T(8,128)(2,1)}), bf16[16,8,1024]{2,1,0:T(8,128)(2,1)S(1)}, u32[]{:S(2)}, u32[]{:S(2)}) %all-to-all-start.10) | async-done | bytes 262176 | tf_op jit(solution)/shard_map/all_to_all | solution.py:14
  309.7 0.8 bitcast_convert_fusion
  (24 shorter events, 0.1 us)
Async XLA Ops:
  7.2 58.2 %all-gather.2.cloned.1.call-start = ((), (), s32[]{:S(2)}) async-start(), calls=%async_computation.13 | async-start | bytes 4456448 | tf_op jit(solution)/shard_map/all_gather | solution.py:107
  7.9 8.4 %copy-start.1 = (bf16[394,1024]{1,0:T(8,128)(2,1)S(1)}, bf16[394,1024]{1,0:T(8,128)(2,1)}, u32[]{:S(2)}) copy-start(bf16[394,1024]{1,0:T(8,128)(2,1)} %param.9) | copy-start | bytes 2420740
  10.5 33.8 %all-to-all-start = ((bf16[8,128,1024]{2,1,0:T(8,128)(2,1)}), bf16[8,128,1024]{2,1,0:T(8,128)(2,1)S(1)}, u32[]{:S(2)}, u32[]{:S(2)}) async-start(bf16[8,128,1024]{2,1,0:T(8,128)(2,1)} %broadcast_in_dim.36), calls=%async_computation | async-start | bytes 4194304 | tf_op jit(solution)/shard_map/all_to_all | solution.py:14
  52.4 13.0 %copy-start.4 = (f32[1,1024]{1,0:T(1,128)S(1)}, f32[1,1024]{1,0:T(1,128)}, u32[]{:S(2)}) copy-start(f32[1,1024]{1,0:T(1,128)} %param.13) | copy-start | bytes 12292
  52.4 13.0 %copy-start.5 = (f32[1024]{0:T(1024)S(1)}, f32[1024]{0:T(1024)}, u32[]{:S(2)}) copy-start(f32[1024]{0:T(1024)} %param.10) | copy-start | bytes 12292
  65.4 4.4 %copy-start.2 = (bf16[2,8,128,1024]{3,2,0,1:T(8,128)(2,1)S(1)}, bf16[2,8,128,1024]{3,2,0,1:T(8,128)(2,1)}, u32[]{:S(2)}) copy-start(bf16[2,8,128,1024]{3,2,0,1:T(8,128)(2,1)} %copy.27) | copy-start | bytes 12582916
  65.4 4.4 %copy-start.3 = (bf16[1,394,1024]{2,1,0:T(8,128)(2,1)S(1)}, bf16[1,394,1024]{2,1,0:T(8,128)(2,1)}, u32[]{:S(2)}) copy-start(bf16[1,394,1024]{2,1,0:T(8,128)(2,1)} %param.17) | copy-start | bytes 2420740
  65.4 4.4 %copy-start.7 = (f32[1,2048]{1,0:T(1,128)S(1)}, f32[1,2048]{1,0:T(1,128)}, u32[]{:S(2)}) copy-start(f32[1,2048]{1,0:T(1,128)} %param.14) | copy-start | bytes 24580
  65.4 4.4 %copy-start.8 = (f32[1,2048]{1,0:T(1,128)S(1)}, f32[1,2048]{1,0:T(1,128)}, u32[]{:S(2)}) copy-start(f32[1,2048]{1,0:T(1,128)} %param.15) | copy-start | bytes 24580
  69.7 2.4 copy-start.9
  81.4 4.6 %copy-start.6 = (bf16[1024,2048]{1,0:T(8,128)(2,1)S(1)}, bf16[1024,2048]{1,0:T(8,128)(2,1)}, u32[]{:S(2)}) copy-start(bf16[1024,2048]{1,0:T(8,128)(2,1)} %all-gather.2.cloned.1.call-done) | copy-start | bytes 12582916
  93.4 10.4 %all-to-all-start.3 = ((bf16[2,8,64,2048]{3,2,1,0:T(8,128)(2,1)}), bf16[2,8,64,2048]{3,2,1,0:T(8,128)(2,1)}, u32[]{:S(2)}, u32[]{:S(2)}) async-start(bf16[2,8,64,2048]{3,2,1,0:T(8,128)(2,1)} %bitcast.50), calls=%async_computation.3 | async-start | bytes 8388608 | tf_op jit(solution)/shard_map/all_to_all | solution.py:36
  116.7 28.3 %all-to-all-start.11 = ((f32[16,1,7168]{2,1,0:T(1,128)}), f32[16,1,7168]{2,1,0:T(1,128)S(1)}, u32[]{:S(2)}, u32[]{:S(2)}) async-start(f32[16,1,7168]{2,1,0:T(1,128)} %broadcast_in_dim.40), calls=%async_computation.11 | async-start | bytes 917504 | tf_op jit(solution)/shard_map/all_to_all | solution.py:14
  145.0 20.5 %all-to-all-start.2 = ((bf16[16,394,64]{1,2,0:T(8,128)(2,1)}), bf16[16,394,64]{1,2,0:T(8,128)(2,1)S(1)}, u32[]{:S(2)}, u32[]{:S(2)}) async-start(bf16[16,394,64]{1,2,0:T(8,128)(2,1)} %bitcast.9), calls=%async_computation.2 | async-start | bytes 2097152 | tf_op jit(solution)/shard_map/all_to_all | solution.py:36
  166.2 10.0 %all-to-all-start.12 = ((f32[16,1,1024]{2,1,0:T(1,128)}), f32[16,1,1024]{2,1,0:T(1,128)S(1)}, u32[]{:S(2)}, u32[]{:S(2)}) async-start(f32[16,1,1024]{2,1,0:T(1,128)} %broadcast_in_dim.45), calls=%async_computation.12 | async-start | bytes 131072 | tf_op jit(solution)/shard_map/all_to_all | solution.py:14
  176.2 31.5 %all-to-all-start.4 = ((bf16[8,64,2048]{2,1,0:T(8,128)(2,1)}), bf16[8,64,2048]{2,1,0:T(8,128)(2,1)S(1)}, u32[]{:S(2)}, u32[]{:S(2)}) async-start(bf16[8,64,2048]{2,1,0:T(8,128)(2,1)} %reduce_sum.188), calls=%async_computation.4 | async-start | bytes 4194304 | tf_op jit(solution)/shard_map/all_to_all | solution.py:44
  207.7 1.3 copy-start
  209.0 33.2 %all-to-all-start.8 = ((bf16[8,128,1024]{2,1,0:T(8,128)(2,1)}), bf16[8,128,1024]{2,1,0:T(8,128)(2,1)S(1)}, u32[]{:S(2)}, u32[]{:S(2)}) async-start(bf16[8,128,1024]{2,1,0:T(8,128)(2,1)} %reduce_sum.191), calls=%async_computation.8 | async-start | bytes 4194304 | tf_op jit(solution)/shard_map/all_to_all | solution.py:44
  242.2 17.6 %all-to-all-start.5 = ((bf16[16,4,2048]{2,1,0:T(4,128)(2,1)}), bf16[16,4,2048]{2,1,0:T(4,128)(2,1)S(1)}, u32[]{:S(2)}, u32[]{:S(2)}) async-start(bf16[16,4,2048]{2,1,0:T(4,128)(2,1)} %reshape.70), calls=%async_computation.5 | async-start | bytes 524288 | tf_op jit(solution)/shard_map/all_to_all | solution.py:36
  259.9 16.1 %all-to-all-start.9 = ((bf16[16,8,1024]{2,1,0:T(8,128)(2,1)}), bf16[16,8,1024]{2,1,0:T(8,128)(2,1)S(1)}, u32[]{:S(2)}, u32[]{:S(2)}) async-start(bf16[16,8,1024]{2,1,0:T(8,128)(2,1)} %bitcast.14), calls=%async_computation.9 | async-start | bytes 524288 | tf_op jit(solution)/shard_map/all_to_all | solution.py:36
  276.8 16.1 %all-to-all-start.6 = ((bf16[16,4,2048]{2,1,0:T(4,128)(2,1)}), bf16[16,4,2048]{2,1,0:T(4,128)(2,1)S(1)}, u32[]{:S(2)}, u32[]{:S(2)}) async-start(bf16[16,4,2048]{2,1,0:T(4,128)(2,1)} %broadcast_in_dim.38), calls=%async_computation.6 | async-start | bytes 524288 | tf_op jit(solution)/shard_map/all_to_all | solution.py:14
  293.6 16.1 %all-to-all-start.10 = ((bf16[16,8,1024]{2,1,0:T(8,128)(2,1)}), bf16[16,8,1024]{2,1,0:T(8,128)(2,1)S(1)}, u32[]{:S(2)}, u32[]{:S(2)}) async-start(bf16[16,8,1024]{2,1,0:T(8,128)(2,1)} %broadcast_in_dim.39), calls=%async_computation.10 | async-start | bytes 524288 | tf_op jit(solution)/shard_map/all_to_all | solution.py:14
Sparse Core Ops, SparseCore 0:
  9.8 55.4 all-gather.1
where the time goes:
time: 319 us; the launch traced here: 317 us
  waiting for transfers between devices  157 us (49%)
  starting transfers between devices  60.5 us (19%)
  matrix products  25.6 us (8%)
  local copies, waits for them, and re-layouts  21.3 us (7%)
  blocking collectives  19.4 us (6%)
  other arithmetic  18.9 us (6%)
  between operations  14.3 us (4%)
    all_to_all x5, waiting for transfers between devices, sent_to_all(): return lax.all_to_all(copies, axis, split_axis=0, concat_axis=0, tiled=True)  64.2 us
    all_to_all x2, waiting for transfers between devices, summed_rows(): lax.all_to_all(nearer.astype(jnp.bfloat16), far, split_axis=0, concat_axi...  42.3 us
    all_to_all x4, waiting for transfers between devices, sent_and_summed(): lax.all_to_all(tiles, axis, split_axis=0, concat_axis=0, tiled=True)  39.6 us
    all_to_all x5, starting transfers between devices, sent_to_all(): return lax.all_to_all(copies, axis, split_axis=0, concat_axis=0, tiled=True)  27.9 us
    all_to_all x4, starting transfers between devices, sent_and_summed(): lax.all_to_all(tiles, axis, split_axis=0, concat_axis=0, tiled=True)  18.1 us
    all_to_all x2, starting transfers between devices, summed_rows(): lax.all_to_all(nearer.astype(jnp.bfloat16), far, split_axis=0, concat_axi...  14.4 us
    all_to_all x1, blocking collectives, sent_and_summed(): lax.all_to_all(tiles, axis, split_axis=0, concat_axis=0, tiled=True)  11.9 us
    reduce_sum x5, other arithmetic, sent_and_summed(): return arrived.astype(jnp.float32).sum(axis=0)  11.4 us
  transfers between devices with their start and end apart: 12, of which 10 were waited for; matrix products, arithmetic and copies ran while one was open for 10% of the time, Pallas kernels for 0%

commit v1 on v0

--- a/solution.py
+++ b/solution.py
@@ -104,7 +104,9 @@
     normed = centered * inv_std
     gained = normed * normgain
     scaled_in = (gained * scale_in).astype(jnp.bfloat16)
-    expand_full = lax.all_gather(expand, MEMBER, axis=0, tiled=True)
+    expand_full = jnp.concatenate(
+        lax.all_to_all(jnp.stack([expand] * lax.axis_size(MEMBER)), MEMBER, 0, 0), axis=0
+    )
     project = jnp.dot(scaled_in, expand_full, preferred_element_type=jnp.float32)
     hidden = project * scale_hid
     active, slope = gelu_pair(hidden)

time: 319 us -> 355 us (1.11)
  blocking collectives: 19.4 us -> 51.3 us
  between operations: 14.3 us -> 0.89 us
  waiting for transfers between devices: 157 us -> 169 us
    all_to_all x0 -> x1, waiting for transfers between devices: none -> 50.2 us  [body(): lax.all_to_all(jnp.stack([expand] * lax.axis_size(MEMBER)), MEMBER, 0, 0)]
    all_to_all x1 -> x2, blocking collectives: 7.52 us -> 39.4 us  [sent_to_all(): return lax.all_to_all(copies, axis, split_axis=0, concat_axis=0, tiled=True)]
    all_to_all x5 -> x4, waiting for transfers between devices: 64.2 us -> 36.7 us  [sent_to_all(): return lax.all_to_all(copies, axis, split_axis=0, concat_axis=0, tiled=True)]
    all_gather x1 -> x0, waiting for transfers between devices: 10.6 us -> none  [body(): expand_full = lax.all_gather(expand, MEMBER, axis=0, tiled=True)]
    all_to_all x0 -> x1, starting transfers between devices: none -> 5.9 us  [body(): lax.all_to_all(jnp.stack([expand] * lax.axis_size(MEMBER)), MEMBER, 0, 0)]
    all_to_all x5 -> x4, starting transfers between devices: 27.9 us -> 22.2 us  [sent_to_all(): return lax.all_to_all(copies, axis, split_axis=0, concat_axis=0, tiled=True)]
  transfers between devices with their start and end apart: 12 -> 11, of which waited for: 10 -> 9; matrix products, arithmetic and copies ran while one was open for 10% -> 9% of each run, Pallas kernels for 0% -> 0%
where the time goes in v1:
time: 355 us; the launch traced here: 353 us
  waiting for transfers between devices  169 us (48%)
  starting transfers between devices  60.4 us (17%)
  blocking collectives  51.3 us (14%)
  matrix products  28 us (8%)
  local copies, waits for them, and re-layouts  24.8 us (7%)
  other arithmetic  18.9 us (5%)
    all_to_all x1, waiting for transfers between devices, body(): lax.all_to_all(jnp.stack([expand] * lax.axis_size(MEMBER)), MEMBER, 0, 0)  50.2 us
    all_to_all x2, waiting for transfers between devices, summed_rows(): lax.all_to_all(nearer.astype(jnp.bfloat16), far, split_axis=0, concat_axi...  42.3 us
    all_to_all x4, waiting for transfers between devices, sent_and_summed(): lax.all_to_all(tiles, axis, split_axis=0, concat_axis=0, tiled=True)  39.6 us
    all_to_all x2, blocking collectives, sent_to_all(): return lax.all_to_all(copies, axis, split_axis=0, concat_axis=0, tiled=True)  39.4 us
    all_to_all x4, waiting for transfers between devices, sent_to_all(): return lax.all_to_all(copies, axis, split_axis=0, concat_axis=0, tiled=True)  36.7 us
    all_to_all x4, starting transfers between devices, sent_to_all(): return lax.all_to_all(copies, axis, split_axis=0, concat_axis=0, tiled=True)  22.2 us
    all_to_all x4, starting transfers between devices, sent_and_summed(): lax.all_to_all(tiles, axis, split_axis=0, concat_axis=0, tiled=True)  17.9 us
    all_to_all x2, starting transfers between devices, summed_rows(): lax.all_to_all(nearer.astype(jnp.bfloat16), far, split_axis=0, concat_axi...  14.4 us
  transfers between devices with their start and end apart: 11, of which 9 were waited for; matrix products, arithmetic and copies ran while one was open for 9% of the time, Pallas kernels for 0%

profile of v1, /device:TPU:8, one launch (start us, length us, event | category | flops | bytes accessed | tf_op | source)
XLA Modules:
  0.0 353.1 jit_solution(1773057368930031989)
XLA Ops:
  0.6 1.2 broadcast_in_dim.36
  1.8 31.0 %all_to_all.72 = bf16[8,128,1024]{2,1,0:T(8,128)(2,1)S(1)} all-to-all(bf16[8,128,1024]{2,1,0:T(8,128)(2,1)S(1)} %broadcast_in_dim.36), channel_id=1, replica_groups=mesh['member_0'=2,'member_1'=4,'member_2'=2,'dp'=16] {'member_0','member..., dimensions={0} | all-to-all | bytes 4194304 | tf_op jit(solution)/shard_map/all_to_all | solution.py:14
  32.9 0.6 broadcast_in_dim.37
  33.5 0.0 copy-start.4
  33.5 8.3 %all_to_all.73 = bf16[2,8,128,1024]{3,2,1,0:T(8,128)(2,1)} all-to-all(bf16[2,8,128,1024]{3,2,1,0:T(8,128)(2,1)S(1)} %broadcast_in_dim.37), channel_id=1, replica_groups=mesh['member_0'=2,'member_1'=4,'member_2'=2,'dp'=16] {'member_2'}, dimensions={0} | all-to-all | bytes 8388608 | tf_op jit(solution)/shard_map/all_to_all | solution.py:14
  41.8 2.5 stack.2
  44.3 5.9 %all-to-all-start.2 = ((bf16[16,64,2048]{2,1,0:T(8,128)(2,1)}), bf16[16,64,2048]{2,1,0:T(8,128)(2,1)}, u32[]{:S(2)}, u32[]{:S(2)}) async-start(bf16[16,64,2048]{2,1,0:T(8,128)(2,1)} %stack.2), calls=%async_computation.2 | async-start | bytes 8388608 | tf_op jit(solution)/shard_map/all_to_all | solution.py:108
  50.2 0.2 convert_reduce_fusion
  50.4 0.4 fusion.23
  50.8 0.0 copy-start.5
  50.8 0.0 copy-start.6
  50.8 4.8 %copy.27 = bf16[2,8,128,1024]{3,2,0,1:T(8,128)(2,1)} copy(bf16[2,8,128,1024]{3,2,1,0:T(8,128)(2,1)} %all_to_all.73) | data formatting | bytes 8388608 | tf_op jit(solution)/shard_map/all_to_all | solution.py:14
  55.6 50.2 %all-to-all-done.2 = bf16[16,64,2048]{2,1,0:T(8,128)(2,1)} async-done(((bf16[16,64,2048]{2,1,0:T(8,128)(2,1)}), bf16[16,64,2048]{2,1,0:T(8,128)(2,1)}, u32[]{:S(2)}, u32[]{:S(2)}) %all-to-all-start.2) | async-done | bytes 4194336 | tf_op jit(solution)/shard_map/all_to_all | solution.py:108
  105.8 0.0 copy-start.7
  105.8 0.0 copy-start.8
  105.8 4.3 %fusion.37 = f32[394,2048]{1,0:T(8,128)S(1)} fusion(bf16[1024,2048]{1,0:T(8,128)(2,1)} %bitcast.7, bf16[394,1024]{1,0:T(8,128)(2,1)S(1)} %copy-done.1, f32[1024]{0:T(1024)S(1)} %bitcast.61, f32[1024]{0:T(1024)S(1)} %copy-done.6, f32[394]{0:T(512)S(1)} %add_rsqrt_fusion, f32[394]{0:T(512)S(1)} %broadcast_multiply_fusion.2), kind=kOutput, calls=%fused_computation.60 | convolution fusion | flops 1654976512 | bytes 8240208 | tf_op jit(solution)/shard_map/dot_general | solution.py:110
  110.2 0.0 copy-start.9
  110.2 2.4 fusion.26
  112.6 4.2 %multiply_reduce_fusion = (f32[2048]{0:T(1024)S(1)}, f32[2048]{0:T(1024)S(1)}, f32[394,2048]{1,0:T(8,128)S(1)}) fusion(f32[394,2048]{1,0:T(8,128)S(1)} %fusion.37, f32[2048]{0:T(1024)S(1)} %bitcast.66, f32[2048]{0:T(1024)S(1)} %bitcast.71, bf16[2048,1024]{1,0:T(8,128)(2,1)S(1)} %bitcast.54, bf16[1,394,1024]{2,1,0:T(8,128)(2,1)S(1)} %copy-done.3, ...), kind=kOutput, calls=%fused_computation.12 | convolution fusion | flops 1673934848 | bytes 11493376 | tf_op jit(solution)/shard_map/dot_general | solution.py:118
  116.8 7.6 %fusion.22 = (f32[1024]{0:T(1024)S(1)}, f32[394]{0:T(512)S(1)}, f32[1024]{0:T(1024)S(1)}, f32[394]{0:T(512)S(1)}, f32[394,1024]{1,0:T(8,128)}) fusion(bf16[394,1024]{1,0:T(8,128)(2,1)S(1)} %copy-done.1, f32[1024]{0:T(1024)S(1)} %bitcast.62, f32[394]{0:T(512)S(1)} %add_rsqrt_fusion, f32[394]{0:T(512)S(1)} %broadcast_multiply_fusion.2, ...), kind=kOutput, calls=%fused_computation.37 | convolution fusion | flops 1675549952 | bytes 13109408 | tf_op jit(solution)/shard_map/dot_general | solution.py:142
  124.4 4.5 %convolution_convert_fusion.1 = bf16[1024,2048]{1,0:T(8,128)(2,1)S(1)} fusion(f32[2048]{0:T(1024)S(1)} %bitcast.68, bf16[394,1024]{1,0:T(8,128)(2,1)S(1)} %copy-done.1, f32[1024]{0:T(1024)S(1)} %bitcast.63, f32[1024]{0:T(1024)S(1)} %copy-done.6, f32[394]{0:T(512)S(1)} %add_rsqrt_fusion, f32[394]{0:T(512)S(1)} %broadcast_multiply_fusion.2, ...), kind=kOutput, calls=%fused_computation.5 | convolution fusion | flops 1674825728 | bytes 11484240 | tf_op jit(solution)/shard_map/dot_general | solution.py:89
  128.9 5.0 %convolution_convert_fusion = bf16[2048,1024]{1,0:T(8,128)(2,1)} fusion(bf16[1,394,1024]{2,1,0:T(8,128)(2,1)S(1)} %copy-done.3, f32[1024]{0:T(1024)S(1)} %bitcast.76, f32[2048]{0:T(1024)S(1)} %bitcast.74, f32[394,2048]{1,0:T(8,128)S(1)} %fusion.37, f32[2048]{0:T(1024)S(1)} %bitcast.69), kind=kOutput, calls=%fused_computation.4 | convolution fusion | flops 1664739328 | bytes 8249344 | tf_op jit(solution)/shard_map/dot_general | solution.py:89
  133.9 2.3 copy.45
  136.2 5.6 %all-to-all-start.4 = ((bf16[2,8,64,2048]{3,2,1,0:T(8,128)(2,1)}), bf16[2,8,64,2048]{3,2,1,0:T(8,128)(2,1)}, u32[]{:S(2)}, u32[]{:S(2)}) async-start(bf16[2,8,64,2048]{3,2,1,0:T(8,128)(2,1)} %bitcast.51), calls=%async_computation.4 | async-start | bytes 8388608 | tf_op jit(solution)/shard_map/all_to_all | solution.py:36
  141.8 4.8 %copy.44 = bf16[8,2,128,1024]{3,2,0,1:T(8,128)(2,1)} copy(bf16[8,2,128,1024]{3,2,1,0:T(8,128)(2,1)} %bitcast.55) | data formatting | bytes 8388608 | tf_op jit(solution)/shard_map/reshape;reshape | solution.py:31
  146.6 0.0 all-to-all-done.4
  146.6 11.9 %all_to_all.74 = bf16[2,8,128,1024]{3,2,1,0:T(8,128)(2,1)} all-to-all(bf16[2,8,128,1024]{3,2,1,0:T(8,128)(2,1)} %bitcast.52), channel_id=1, replica_groups=mesh['member_0'=2,'member_1'=4,'member_2'=2,'dp'=16] {'member_2'}, dimensions={0} | all-to-all | bytes 8388608 | tf_op jit(solution)/shard_map/all_to_all | solution.py:36
  158.5 1.0 broadcast_in_dim.40
  159.5 10.3 %all-to-all-start.12 = ((f32[16,1,7168]{2,1,0:T(1,128)}), f32[16,1,7168]{2,1,0:T(1,128)S(1)}, u32[]{:S(2)}, u32[]{:S(2)}) async-start(f32[16,1,7168]{2,1,0:T(1,128)} %broadcast_in_dim.40), calls=%async_computation.12 | async-start | bytes 917504 | tf_op jit(solution)/shard_map/all_to_all | solution.py:14
  169.8 2.2 fusion.24
  172.0 1.4 copy.28
  173.3 14.5 %all-to-all-done.12 = f32[16,1,7168]{2,1,0:T(1,128)S(1)} async-done(((f32[16,1,7168]{2,1,0:T(1,128)}), f32[16,1,7168]{2,1,0:T(1,128)S(1)}, u32[]{:S(2)}, u32[]{:S(2)}) %all-to-all-start.12) | async-done | bytes 458784 | tf_op jit(solution)/shard_map/all_to_all | solution.py:14
  187.9 5.2 %all-to-all-start.3 = ((bf16[16,394,64]{1,2,0:T(8,128)(2,1)}), bf16[16,394,64]{1,2,0:T(8,128)(2,1)S(1)}, u32[]{:S(2)}, u32[]{:S(2)}) async-start(bf16[16,394,64]{1,2,0:T(8,128)(2,1)} %bitcast.10), calls=%async_computation.3 | async-start | bytes 2097152 | tf_op jit(solution)/shard_map/all_to_all | solution.py:36
  193.1 0.3 reduce_sum.199
  193.4 0.6 fusion.41
  194.0 14.2 %all-to-all-done.3 = bf16[16,394,64]{1,2,0:T(8,128)(2,1)S(1)} async-done(((bf16[16,394,64]{1,2,0:T(8,128)(2,1)}), bf16[16,394,64]{1,2,0:T(8,128)(2,1)S(1)}, u32[]{:S(2)}, u32[]{:S(2)}) %all-to-all-start.3) | async-done | bytes 806944 | tf_op jit(solution)/shard_map/all_to_all | solution.py:36
  208.2 0.7 broadcast_in_dim.45
  208.9 4.8 %all-to-all-start.13 = ((f32[16,1,1024]{2,1,0:T(1,128)}), f32[16,1,1024]{2,1,0:T(1,128)S(1)}, u32[]{:S(2)}, u32[]{:S(2)}) async-start(f32[16,1,1024]{2,1,0:T(1,128)} %broadcast_in_dim.45), calls=%async_computation.13 | async-start | bytes 131072 | tf_op jit(solution)/shard_map/all_to_all | solution.py:14
  213.7 5.2 %reduce_sum.188 = bf16[8,64,2048]{2,1,0:T(8,128)(2,1)} reduce(bf16[2,8,64,2048]{3,2,1,0:T(8,128)(2,1)} %all-to-all-done.4, bf16[]{:T(256)} %constant.28.clone.1), dimensions={0}, to_apply=%region_5.0 | reduce | flops 1048576 | bytes 6291458 | tf_op jit(solution)/shard_map/reduce_sum | solution.py:37
  218.8 5.7 %all-to-all-start.5 = ((bf16[8,64,2048]{2,1,0:T(8,128)(2,1)}), bf16[8,64,2048]{2,1,0:T(8,128)(2,1)S(1)}, u32[]{:S(2)}, u32[]{:S(2)}) async-start(bf16[8,64,2048]{2,1,0:T(8,128)(2,1)} %reduce_sum.188), calls=%async_computation.5 | async-start | bytes 4194304 | tf_op jit(solution)/shard_map/all_to_all | solution.py:44
  224.6 5.2 %reduce_sum.191 = bf16[8,128,1024]{2,1,0:T(8,128)(2,1)} reduce(bf16[2,8,128,1024]{3,2,1,0:T(8,128)(2,1)} %all_to_all.74, bf16[]{:T(256)} %constant.28.clone.1), dimensions={0}, to_apply=%region_8.0 | reduce | flops 1048576 | bytes 6291458 | tf_op jit(solution)/shard_map/reduce_sum | solution.py:37
  229.8 20.5 %all-to-all-done.5 = bf16[8,64,2048]{2,1,0:T(8,128)(2,1)S(1)} async-done(((bf16[8,64,2048]{2,1,0:T(8,128)(2,1)}), bf16[8,64,2048]{2,1,0:T(8,128)(2,1)S(1)}, u32[]{:S(2)}, u32[]{:S(2)}) %all-to-all-start.5) | async-done | bytes 2097184 | tf_op jit(solution)/shard_map/all_to_all | solution.py:44
  250.3 1.3 copy-done
  251.6 8.7 %all-to-all-start.9 = ((bf16[8,128,1024]{2,1,0:T(8,128)(2,1)}), bf16[8,128,1024]{2,1,0:T(8,128)(2,1)S(1)}, u32[]{:S(2)}, u32[]{:S(2)}) async-start(bf16[8,128,1024]{2,1,0:T(8,128)(2,1)} %reduce_sum.191), calls=%async_computation.9 | async-start | bytes 4194304 | tf_op jit(solution)/shard_map/all_to_all | solution.py:44
  260.3 2.0 reduce_sum.189
  262.3 0.8 reshape.76
  263.1 21.8 %all-to-all-done.9 = bf16[8,128,1024]{2,1,0:T(8,128)(2,1)S(1)} async-done(((bf16[8,128,1024]{2,1,0:T(8,128)(2,1)}), bf16[8,128,1024]{2,1,0:T(8,128)(2,1)S(1)}, u32[]{:S(2)}, u32[]{:S(2)}) %all-to-all-start.9) | async-done | bytes 2097184 | tf_op jit(solution)/shard_map/all_to_all | solution.py:44
  284.9 3.5 %all-to-all-start.6 = ((bf16[16,4,2048]{2,1,0:T(4,128)(2,1)}), bf16[16,4,2048]{2,1,0:T(4,128)(2,1)S(1)}, u32[]{:S(2)}, u32[]{:S(2)}) async-start(bf16[16,4,2048]{2,1,0:T(4,128)(2,1)} %reshape.76), calls=%async_computation.6 | async-start | bytes 524288 | tf_op jit(solution)/shard_map/all_to_all | solution.py:36
  288.4 1.1 reduce_sum.192
  289.5 13.0 %all-to-all-done.6 = bf16[16,4,2048]{2,1,0:T(4,128)(2,1)S(1)} async-done(((bf16[16,4,2048]{2,1,0:T(4,128)(2,1)}), bf16[16,4,2048]{2,1,0:T(4,128)(2,1)S(1)}, u32[]{:S(2)}, u32[]{:S(2)}) %all-to-all-start.6) | async-done | bytes 262176 | tf_op jit(solution)/shard_map/all_to_all | solution.py:36
  302.5 3.5 %all-to-all-start.10 = ((bf16[16,8,1024]{2,1,0:T(8,128)(2,1)}), bf16[16,8,1024]{2,1,0:T(8,128)(2,1)S(1)}, u32[]{:S(2)}, u32[]{:S(2)}) async-start(bf16[16,8,1024]{2,1,0:T(8,128)(2,1)} %bitcast.15), calls=%async_computation.10 | async-start | bytes 524288 | tf_op jit(solution)/shard_map/all_to_all | solution.py:36
  306.0 0.1 reduce_sum.190
  306.2 12.4 %all-to-all-done.10 = bf16[16,8,1024]{2,1,0:T(8,128)(2,1)S(1)} async-done(((bf16[16,8,1024]{2,1,0:T(8,128)(2,1)}), bf16[16,8,1024]{2,1,0:T(8,128)(2,1)S(1)}, u32[]{:S(2)}, u32[]{:S(2)}) %all-to-all-start.10) | async-done | bytes 262176 | tf_op jit(solution)/shard_map/all_to_all | solution.py:36
  318.6 0.8 broadcast_in_dim.38
  319.4 3.5 %all-to-all-start.7 = ((bf16[16,4,2048]{2,1,0:T(4,128)(2,1)}), bf16[16,4,2048]{2,1,0:T(4,128)(2,1)S(1)}, u32[]{:S(2)}, u32[]{:S(2)}) async-start(bf16[16,4,2048]{2,1,0:T(4,128)(2,1)} %broadcast_in_dim.38), calls=%async_computation.7 | async-start | bytes 524288 | tf_op jit(solution)/shard_map/all_to_all | solution.py:14
  323.0 12.5 %all-to-all-done.7 = bf16[16,4,2048]{2,1,0:T(4,128)(2,1)S(1)} async-done(((bf16[16,4,2048]{2,1,0:T(4,128)(2,1)}), bf16[16,4,2048]{2,1,0:T(4,128)(2,1)S(1)}, u32[]{:S(2)}, u32[]{:S(2)}) %all-to-all-start.7) | async-done | bytes 262176 | tf_op jit(solution)/shard_map/all_to_all | solution.py:14
  335.5 0.7 broadcast_in_dim.39
  336.2 3.5 %all-to-all-start.11 = ((bf16[16,8,1024]{2,1,0:T(8,128)(2,1)}), bf16[16,8,1024]{2,1,0:T(8,128)(2,1)S(1)}, u32[]{:S(2)}, u32[]{:S(2)}) async-start(bf16[16,8,1024]{2,1,0:T(8,128)(2,1)} %broadcast_in_dim.39), calls=%async_computation.11 | async-start | bytes 524288 | tf_op jit(solution)/shard_map/all_to_all | solution.py:14
  339.8 0.8 reduce_sum.187
  340.6 0.6 fusion.42
  341.2 0.6 reduce_sum.200
  341.8 0.8 reshape.79
  342.6 9.7 %all-to-all-done.11 = bf16[16,8,1024]{2,1,0:T(8,128)(2,1)S(1)} async-done(((bf16[16,8,1024]{2,1,0:T(8,128)(2,1)}), bf16[16,8,1024]{2,1,0:T(8,128)(2,1)S(1)}, u32[]{:S(2)}, u32[]{:S(2)}) %all-to-all-start.11) | async-done | bytes 262176 | tf_op jit(solution)/shard_map/all_to_all | solution.py:14
  352.3 0.8 bitcast_convert_fusion
  (23 shorter events, 0.1 us)
Async XLA Ops:
  33.5 8.4 %copy-start.4 = (bf16[64,2048]{1,0:T(8,128)(2,1)S(1)}, bf16[64,2048]{1,0:T(8,128)(2,1)}, u32[]{:S(2)}) copy-start(bf16[64,2048]{1,0:T(8,128)(2,1)} %param.11) | copy-start | bytes 786436
  44.3 5.9 %copy-start.1 = (bf16[394,1024]{1,0:T(8,128)(2,1)S(1)}, bf16[394,1024]{1,0:T(8,128)(2,1)}, u32[]{:S(2)}) copy-start(bf16[394,1024]{1,0:T(8,128)(2,1)} %param.9) | copy-start | bytes 2420740
  44.3 61.4 %all-to-all-start.2 = ((bf16[16,64,2048]{2,1,0:T(8,128)(2,1)}), bf16[16,64,2048]{2,1,0:T(8,128)(2,1)}, u32[]{:S(2)}, u32[]{:S(2)}) async-start(bf16[16,64,2048]{2,1,0:T(8,128)(2,1)} %stack.2), calls=%async_computation.2 | async-start | bytes 8388608 | tf_op jit(solution)/shard_map/all_to_all | solution.py:108
  50.8 55.0 %copy-start.5 = (f32[1,1024]{1,0:T(1,128)S(1)}, f32[1,1024]{1,0:T(1,128)}, u32[]{:S(2)}) copy-start(f32[1,1024]{1,0:T(1,128)} %param.13) | copy-start | bytes 12292
  50.8 55.0 %copy-start.6 = (f32[1024]{0:T(1024)S(1)}, f32[1024]{0:T(1024)}, u32[]{:S(2)}) copy-start(f32[1024]{0:T(1024)} %param.10) | copy-start | bytes 12292
  105.8 4.4 %copy-start.2 = (bf16[2,8,128,1024]{3,2,0,1:T(8,128)(2,1)S(1)}, bf16[2,8,128,1024]{3,2,0,1:T(8,128)(2,1)}, u32[]{:S(2)}) copy-start(bf16[2,8,128,1024]{3,2,0,1:T(8,128)(2,1)} %copy.27) | copy-start | bytes 12582916
  105.8 4.4 %copy-start.3 = (bf16[1,394,1024]{2,1,0:T(8,128)(2,1)S(1)}, bf16[1,394,1024]{2,1,0:T(8,128)(2,1)}, u32[]{:S(2)}) copy-start(bf16[1,394,1024]{2,1,0:T(8,128)(2,1)} %param.17) | copy-start | bytes 2420740
  105.8 4.4 %copy-start.7 = (f32[1,2048]{1,0:T(1,128)S(1)}, f32[1,2048]{1,0:T(1,128)}, u32[]{:S(2)}) copy-start(f32[1,2048]{1,0:T(1,128)} %param.14) | copy-start | bytes 24580
  105.8 4.4 %copy-start.8 = (f32[1,2048]{1,0:T(1,128)S(1)}, f32[1,2048]{1,0:T(1,128)}, u32[]{:S(2)}) copy-start(f32[1,2048]{1,0:T(1,128)} %param.15) | copy-start | bytes 24580
  110.2 2.4 copy-start.9
  136.2 10.4 %all-to-all-start.4 = ((bf16[2,8,64,2048]{3,2,1,0:T(8,128)(2,1)}), bf16[2,8,64,2048]{3,2,1,0:T(8,128)(2,1)}, u32[]{:S(2)}, u32[]{:S(2)}) async-start(bf16[2,8,64,2048]{3,2,1,0:T(8,128)(2,1)} %bitcast.51), calls=%async_computation.4 | async-start | bytes 8388608 | tf_op jit(solution)/shard_map/all_to_all | solution.py:36
  159.5 28.4 %all-to-all-start.12 = ((f32[16,1,7168]{2,1,0:T(1,128)}), f32[16,1,7168]{2,1,0:T(1,128)S(1)}, u32[]{:S(2)}, u32[]{:S(2)}) async-start(f32[16,1,7168]{2,1,0:T(1,128)} %broadcast_in_dim.40), calls=%async_computation.12 | async-start | bytes 917504 | tf_op jit(solution)/shard_map/all_to_all | solution.py:14
  187.9 20.3 %all-to-all-start.3 = ((bf16[16,394,64]{1,2,0:T(8,128)(2,1)}), bf16[16,394,64]{1,2,0:T(8,128)(2,1)S(1)}, u32[]{:S(2)}, u32[]{:S(2)}) async-start(bf16[16,394,64]{1,2,0:T(8,128)(2,1)} %bitcast.10), calls=%async_computation.3 | async-start | bytes 2097152 | tf_op jit(solution)/shard_map/all_to_all | solution.py:36
  208.9 10.0 %all-to-all-start.13 = ((f32[16,1,1024]{2,1,0:T(1,128)}), f32[16,1,1024]{2,1,0:T(1,128)S(1)}, u32[]{:S(2)}, u32[]{:S(2)}) async-start(f32[16,1,1024]{2,1,0:T(1,128)} %broadcast_in_dim.45), calls=%async_computation.13 | async-start | bytes 131072 | tf_op jit(solution)/shard_map/all_to_all | solution.py:14
  218.8 31.5 %all-to-all-start.5 = ((bf16[8,64,2048]{2,1,0:T(8,128)(2,1)}), bf16[8,64,2048]{2,1,0:T(8,128)(2,1)S(1)}, u32[]{:S(2)}, u32[]{:S(2)}) async-start(bf16[8,64,2048]{2,1,0:T(8,128)(2,1)} %reduce_sum.188), calls=%async_computation.5 | async-start | bytes 4194304 | tf_op jit(solution)/shard_map/all_to_all | solution.py:44
  250.3 1.3 copy-start
  251.6 33.2 %all-to-all-start.9 = ((bf16[8,128,1024]{2,1,0:T(8,128)(2,1)}), bf16[8,128,1024]{2,1,0:T(8,128)(2,1)S(1)}, u32[]{:S(2)}, u32[]{:S(2)}) async-start(bf16[8,128,1024]{2,1,0:T(8,128)(2,1)} %reduce_sum.191), calls=%async_computation.9 | async-start | bytes 4194304 | tf_op jit(solution)/shard_map/all_to_all | solution.py:44
  284.9 17.6 %all-to-all-start.6 = ((bf16[16,4,2048]{2,1,0:T(4,128)(2,1)}), bf16[16,4,2048]{2,1,0:T(4,128)(2,1)S(1)}, u32[]{:S(2)}, u32[]{:S(2)}) async-start(bf16[16,4,2048]{2,1,0:T(4,128)(2,1)} %reshape.76), calls=%async_computation.6 | async-start | bytes 524288 | tf_op jit(solution)/shard_map/all_to_all | solution.py:36
  302.5 16.1 %all-to-all-start.10 = ((bf16[16,8,1024]{2,1,0:T(8,128)(2,1)}), bf16[16,8,1024]{2,1,0:T(8,128)(2,1)S(1)}, u32[]{:S(2)}, u32[]{:S(2)}) async-start(bf16[16,8,1024]{2,1,0:T(8,128)(2,1)} %bitcast.15), calls=%async_computation.10 | async-start | bytes 524288 | tf_op jit(solution)/shard_map/all_to_all | solution.py:36
  319.4 16.1 %all-to-all-start.7 = ((bf16[16,4,2048]{2,1,0:T(4,128)(2,1)}), bf16[16,4,2048]{2,1,0:T(4,128)(2,1)S(1)}, u32[]{:S(2)}, u32[]{:S(2)}) async-start(bf16[16,4,2048]{2,1,0:T(4,128)(2,1)} %broadcast_in_dim.38), calls=%async_computation.7 | async-start | bytes 524288 | tf_op jit(solution)/shard_map/all_to_all | solution.py:14
  336.2 16.1 %all-to-all-start.11 = ((bf16[16,8,1024]{2,1,0:T(8,128)(2,1)}), bf16[16,8,1024]{2,1,0:T(8,128)(2,1)S(1)}, u32[]{:S(2)}, u32[]{:S(2)}) async-start(bf16[16,8,1024]{2,1,0:T(8,128)(2,1)} %broadcast_in_dim.39), calls=%async_computation.11 | async-start | bytes 524288 | tf_op jit(solution)/shard_map/all_to_all | solution.py:14
